TPU v7x, 256 devices: a whole 4x4x8 slice. The times are simulated.
256 devices in a mesh: rack: 8 (over x, core), chip: 32 (over y, z).
Axes of the slice: x: 4, y: 4, z: 8, core: 2. Of those that a mesh axis runs over, the one named last changes fastest.
Arguments:
- points: float32 [512, 4, 32, 256], P(('rack', 'chip')), may hold values from -6 to 6
- counts: int32 [512, 256], P(('rack', 'chip')), may hold values from 1 to 32
- cells: int32 [512, 256], P(('rack', 'chip')), may hold values from 0 to 2047, as said below
- pfn_weight: float32 [9, 64], replicated, may hold values from -2 to 2
- pfn_gain: float32 [64], replicated, may hold values from 0.5 to 1.5
- pfn_bias: float32 [64], replicated, may hold values from -3 to 3
- conv_weight: float32 [4, 9, 4096], replicated, may hold values from -0.25 to 0.25
- bn_gain: float32 [4, 64], replicated, may hold values from 0.5 to 1.5
- bn_bias: float32 [4, 64], replicated, may hold values from -3 to 3
- cotangent: float32 [512, 64, 4, 128], P(('rack', 'chip')), may hold values from -0.006 to 0.006
Outputs:
- features: float32 [512, 64, 4, 128], P(('rack', 'chip'))
- conv_grads: float32 [4, 9, 4096], replicated
- norm_grads: float32 [2, 4, 64], replicated
- pillar_grad: float32 [512, 64, 256], P(('rack', 'chip'))
Inputs may be any that keep to these rules, and one draw needn't show every extreme that they name: `cells`: within one sweep no two pillars share a cell.
All inputs are finite; a program needn't handle non-finite values.
Results may differ from a plain program's by a relative error of at most 0.0003.
Values sent between devices are 32-bit elements; how exact they have to be, the bound alone decides.
A program may use at most 128 MiB of HBM per device.

v0:
```python
import functools

import jax
import jax.numpy as jnp
from jax import lax
from jax.experimental import pallas as pl
from jax.experimental.pallas import tpu as pltpu
from jax.sharding import PartitionSpec as P

C = 64
MAXP = 32
LAYERS = 4
PILL = 256
COLS = 128
ROWS = 4
SW = 2
PLANE = ROWS * COLS
POS = SW * PLANE
K9 = 9 * C
EPS = 1e-05
CORES = 2
NZ = 8
NY = 4
LANES = 384
MESH = pl.DeviceIdType.MESH
F32 = jnp.float32
BF16 = jnp.bfloat16


def split(x):
    hi = x.astype(BF16)
    return hi, (x - hi.astype(F32)).astype(BF16)


def mm(a, b):
    return lax.dot_general(a, b, (((1,), (0,)), ((), ())), preferred_element_type=F32)


def mmt(a, b):
    return lax.dot_general(a, b, (((1,), (1,)), ((), ())), preferred_element_type=F32)


def fold(x):
    parts = [x[:, t * COLS : (t + 1) * COLS] for t in range(x.shape[1] // COLS)]
    while len(parts) > 1:
        parts = [parts[t] + parts[t + 1] for t in range(0, len(parts), 2)]
    return parts[0]


def wide(tile, n):
    return jnp.concatenate([tile] * n, axis=1)


def to_row(a, b):
    return jnp.sum(jnp.concatenate([a, b], axis=0).T, axis=0, keepdims=True)


def to_cols(row):
    full = jnp.broadcast_to(row, (2 * C, COLS)).T
    return full[:C], full[C:]


def col_shift(x, step):
    if step == 0:
        return x
    lane = lax.broadcasted_iota(jnp.int32, (x.shape[0], COLS), 1)
    edge = lane == (COLS - 1 if step > 0 else 0)
    turn = COLS - 1 if step > 0 else 1
    tiles = []
    for t in range(x.shape[1] // COLS):
        tile = pltpu.roll(x[:, t * COLS : (t + 1) * COLS], turn, 1)
        tiles.append(jnp.where(edge, 0.0, tile))
    return jnp.concatenate(tiles, axis=1)


def row_shift(x, step):
    if step == 0:
        return x
    none = jnp.zeros((x.shape[0], COLS), x.dtype)
    parts = []
    for s in range(x.shape[1] // PLANE):
        base = s * PLANE
        if step > 0:
            parts += [x[:, base + COLS : base + PLANE], none]
        else:
            parts += [none, x[:, base : base + PLANE - COLS]]
    return jnp.concatenate(parts, axis=1)


def store_taps(x, hi_ref, lo_ref, sign):
    for b in range(3):
        hi, lo = split(col_shift(x, sign * (b - 1)))
        for a in range(3):
            at = pl.ds((3 * a + b) * C, C)
            hi_ref[at, :] = row_shift(hi, sign * (a - 1))
            lo_ref[at, :] = row_shift(lo, sign * (a - 1))


def silu_parts(y):
    sg = 1.0 / (1.0 + jnp.exp(-y))
    return y * sg, sg * (1.0 + y * (1.0 - sg))


def step_kernel(
    size,
    points,
    counts,
    cells,
    pfn_w,
    pfn_g,
    pfn_b,
    w_fwd,
    w_bwd,
    bn_g,
    bn_b,
    cot,
    features,
    grads_out,
    norm_out,
    pillar_out,
    x9h,
    x9l,
    g9h,
    g9l,
    hot,
    xhat,
    slope,
    wf,
    wb,
    w0h,
    w0l,
    par,
    pwc,
    hmax,
    base,
    sq,
    u_ref,
    gy_ref,
    p_src,
    p_buf,
    s_src,
    s_buf,
    dw,
    rs_buf,
    x_src,
    x_buf,
    ag_src,
    full,
    p_send,
    p_recv,
    s_send,
    s_recv,
    g_send,
    g_recv,
):
    nx, ny, nz = size
    ga, gb = CORES * nz, nx * ny
    devices = ga * gb
    rack = lax.axis_index("rack")
    chip = lax.axis_index("chip")
    core = lax.rem(rack, CORES)
    my_x = rack // CORES
    my_z = lax.rem(chip, nz)
    my_y = chip // nz
    me = (core * nz + my_z, my_x * ny + my_y)
    groups = (ga, gb)

    def peer(phase, i):
        if phase == 0:
            return (my_x * CORES + i // nz, my_y * nz + lax.rem(i, nz))
        return ((i // ny) * CORES + core, lax.rem(i, ny) * nz + my_z)

    def each_peer(phase, act):
        def one(d, carry):
            act(lax.rem(me[phase] + d, groups[phase]))
            return carry

        lax.fori_loop(1, groups[phase], one, 0)

    barrier = pltpu.get_barrier_semaphore()
    for phase in range(2):
        each_peer(
            phase,
            lambda i, phase=phase: pl.semaphore_signal(
                barrier, inc=1, device_id=peer(phase, i), device_id_type=MESH
            ),
        )

    def spread(phase, src, buf, send, recv):
        def act(i):
            pltpu.make_async_remote_copy(
                src_ref=src,
                dst_ref=buf.at[me[phase]],
                send_sem=send,
                recv_sem=recv,
                device_id=peer(phase, i),
                device_id_type=MESH,
            ).start()

        each_peer(phase, act)

    def settle(phase, buf, sem):
        part = buf.at[pl.ds(0, groups[phase] - 1)]
        pltpu.make_async_copy(part, part, sem).wait()

    lane = lax.broadcasted_iota(jnp.int32, (1, COLS), 1)
    low = lane < C

    def columns(row_a, row_b):
        return to_cols(jnp.concatenate([row_a, row_b], axis=1))

    w = [pfn_w[f : f + 1, :] for f in range(9)]
    rows = [w[0] + w[4] + w[7], w[1] + w[5] + w[8], w[2] + w[6], w[3]] + w[4:9] + [w[8]]
    for k in range(0, 10, 2):
        pwc[k], pwc[k + 1] = columns(rows[k], rows[k + 1])

    half = lambda x, h: x[:, h * COLS : (h + 1) * COLS]
    slot = lax.broadcasted_iota(jnp.int32, (MAXP, PILL), 0)
    local_n = jnp.sum(counts[...].astype(F32))
    mean_tile = jnp.zeros((C, COLS), F32)
    for s in range(SW):
        n_row = counts[s : s + 1, :]
        n_f = n_row.astype(F32)
        ok = slot < n_row
        sums = [
            jnp.sum(jnp.where(ok, points[s, j], 0.0), axis=0, keepdims=True) for j in range(4)
        ]
        cell = cells[s : s + 1, :]
        col_pos = lax.rem(cell, 2 * COLS).astype(F32) * (1.0 / COLS) - 1.0
        row_pos = (cell // (2 * COLS)).astype(F32) * 0.25 - 1.0
        fixed = [sums[0] / n_f, sums[1] / n_f, sums[2] / n_f, col_pos, row_pos]
        for h in range(2):
            off = jnp.zeros((C, COLS), F32)
            for j in range(5):
                off = off - pwc[4 + j] * half(fixed[j], h)
            base[s, :, h * COLS : (h + 1) * COLS] = off
            acc = off * half(n_f, h)
            for j in range(4):
                acc = acc + pwc[j] * half(sums[j], h)
            mean_tile = mean_tile + acc
    local_mean = jnp.sum(mean_tile, axis=1, keepdims=True) / local_n

    pwc[9] = jnp.broadcast_to(local_mean, (C, COLS))
    for s in range(SW):
        base[s] = base[s] - wide(pwc[9], 2)

    grp = 16

    def channels(g, carry):
        at = pl.ds(pl.multiple_of(g * grp, grp), grp)
        wj = [pwc[j, at, :] for j in range(4)]

        def walk(k8, carry):
            tops, acc = list(carry[:-1]), carry[-1]
            first = pl.multiple_of(k8 * 8, 8)
            for s in range(SW):
                for h in range(2):
                    lanes = slice(h * COLS, (h + 1) * COLS)
                    off = base[s, at, lanes]
                    left = jnp.broadcast_to(counts[s : s + 1, lanes] - first, (grp, COLS))
                    pts = [points[s, j, pl.ds(first, 8), lanes] for j in range(4)]
                    for k in range(8):
                        value = off
                        for j in range(4):
                            value = value + wj[j] * pts[j][k : k + 1, :]
                        ok = left > k
                        top = jnp.where(ok, value, -3e38)
                        tops[2 * s + h] = jnp.maximum(tops[2 * s + h], top)
                        value = jnp.where(ok, value, 0.0)
                        acc = acc + value * value
            return (*tops, acc)

        start = [jnp.full((grp, COLS), -3e38, F32)] * (2 * SW)
        done = lax.fori_loop(0, MAXP // 8, walk, (*start, jnp.zeros((grp, COLS), F32)))
        for s in range(SW):
            for h in range(2):
                hmax[s, at, h * COLS : (h + 1) * COLS] = done[2 * s + h] + pwc[9, at, :]
        sq[at, :] = done[-1]
        return carry

    lax.fori_loop(0, C // grp, channels, 0)

    row = to_row(mean_tile, sq[...])
    row = jnp.where(low, row / local_n, row)
    payload = jnp.concatenate([row, jnp.full((1, COLS), local_n, F32)], axis=1)

    def merge_pfn(v):
        a, n = v[:, :, :COLS], v[:, :, COLS:]
        total = jnp.sum(n, axis=0)
        avg = jnp.sum(n * a, axis=0) / total
        dev = a - avg[None]
        spread_sq = jnp.sum(n * dev * dev, axis=0)
        both = jnp.where(low, avg, jnp.sum(a, axis=0) + pltpu.roll(spread_sq, C, 1))
        return jnp.concatenate([both, total], axis=1)

    pl.semaphore_wait(barrier, ga + gb - 2)
    p_src[0] = payload
    p_buf[0, me[0]] = payload
    spread(0, p_src.at[0], p_buf.at[0], p_send.at[0], p_recv.at[0])

    for s in range(SW):
        cell = cells[s : s + 1, :]
        r, c = cell // (2 * COLS), lax.rem(cell, 2 * COLS)
        spot = (
            (lax.rem(r, 2) * 2 + lax.rem(c, 2)) * PLANE + (r // 2) * COLS + c // 2
        )

        def fill(t, carry, s=s, spot=spot):
            ids = lax.broadcasted_iota(jnp.int32, (COLS, PILL), 0) + t * COLS
            hit = jnp.where(ids == spot, 1.0, 0.0)
            hot[s, pl.ds(pl.multiple_of(t * COLS, COLS), COLS), :] = hit.astype(BF16)
            return carry

        lax.fori_loop(0, 4 * PLANE // COLS, fill, 0)
    par[0], par[1] = columns(pfn_g[...], pfn_b[...])
    for l in range(LAYERS):
        par[2 + 2 * l], par[3 + 2 * l] = columns(bn_g[l : l + 1, :], bn_b[l : l + 1, :])

    def load_weights(l, carry):
        wf[l, :C, :], wf[l, C:, :] = split(w_fwd[l])
        wb[l, :C, :], wb[l, C:, :] = split(w_bwd[l])
        return carry

    lax.fori_loop(0, LAYERS, load_weights, 0)
    tap = lax.broadcasted_iota(jnp.int32, (C, K9), 1) // C
    parity = jnp.where(tap // 3 == 1, 0, 2) + jnp.where(lax.rem(tap, 3) == 1, 0, 1)
    for ph in range(4):
        hi, lo = split(jnp.where(parity == ph, w_bwd[0], 0.0))
        w0h[ph * C : (ph + 1) * C, :] = hi
        w0l[ph * C : (ph + 1) * C, :] = lo
    for l in range(LAYERS):
        dw[l, :, K9:] = jnp.zeros((C, 2 * LANES - K9), F32)

    settle(0, p_buf.at[0], p_recv.at[0])
    payload = merge_pfn(p_buf[0, pl.ds(0, ga)])
    p_src[1] = payload
    p_buf[1, me[1]] = payload
    spread(1, p_src.at[1], p_buf.at[1], p_send.at[1], p_recv.at[1])
    settle(1, p_buf.at[1], p_recv.at[1])
    payload = merge_pfn(p_buf[1, pl.ds(0, gb)])
    row, total = payload[:, :COLS], payload[:, COLS:]
    mean_c, inv_c = to_cols(jnp.where(low, row, lax.rsqrt(row / total + EPS)))
    scale = par[0] * inv_c

    for s in range(SW):
        pillar = jnp.concatenate(
            [
                jnp.maximum((half(hmax[s], h) - mean_c) * scale + par[1], 0.0)
                for h in range(2)
            ],
            axis=1,
        )
        hi, lo = split(pillar)
        both = jnp.concatenate([hi, lo], axis=0)
        lanes = slice(s * PLANE, (s + 1) * PLANE)
        for pr in range(2):
            for pc in range(2):
                ph = 2 * pr + pc
                plane = mmt(both, hot[s, ph * PLANE : (ph + 1) * PLANE, :])
                for b in (0, 2) if pc else (1,):
                    moved = col_shift(plane, -1 if b == 0 else 0).astype(BF16)
                    for a in (0, 2) if pr else (1,):
                        out = row_shift(moved, -1 if a == 0 else 0)
                        at = slice((3 * a + b) * C, (3 * a + b + 1) * C)
                        x9h[0, at, lanes] = out[:C]
                        x9l[0, at, lanes] = out[C:]

    def send_stat(rnd, phase, row):
        s_src[rnd, phase] = row
        s_buf[rnd, phase, me[phase]] = row
        spread(
            phase,
            s_src.at[rnd, phase],
            s_buf.at[rnd, phase],
            s_send.at[rnd, phase],
            s_recv.at[rnd, phase],
        )

    def take_stat(rnd, phase):
        settle(phase, s_buf.at[rnd, phase], s_recv.at[rnd, phase])
        return s_buf[rnd, phase, pl.ds(0, groups[phase])]

    def merge_norm(v, count):
        total = jnp.sum(v, axis=0)
        avg = total / v.shape[0]
        dev = v - avg[None]
        spread_sq = jnp.sum(dev * dev, axis=0) * count
        return jnp.where(low, avg, total + pltpu.roll(spread_sq, C, 1))

    def norm_layer(l, rnd):
        xh = x9h.at[l]
        xl = x9l.at[l]
        wide_z = mm(wf[l], xh[...])
        z = wide_z[:C] + wide_z[C:] + mm(wf[l, :C, :], xl[...])
        part = fold(z)
        m = jnp.sum(part, axis=1, keepdims=True) * (1.0 / POS)
        dev = z - m
        row = to_row(part, fold(dev * dev))
        send_stat(rnd, 0, jnp.where(low, row * (1.0 / POS), row))
        row = merge_norm(take_stat(rnd, 0), float(POS))
        send_stat(rnd, 1, row)
        row = merge_norm(take_stat(rnd, 1), float(POS * ga))
        mean_col, inv_col = to_cols(
            jnp.where(low, row, lax.rsqrt(row * (1.0 / (POS * devices)) + EPS))
        )
        normed = (z - wide(mean_col, POS // COLS)) * wide(inv_col, POS // COLS)
        gain, bias = par[2 + 2 * l], par[3 + 2 * l]
        y = wide(gain, POS // COLS) * normed + wide(bias, POS // COLS)
        act, slp = silu_parts(y)
        xhat[l] = normed
        slope[l] = slp
        par[10 + l] = gain * inv_col
        return act

    store_taps(norm_layer(0, 0), x9h.at[1], x9l.at[1], 1)

    def middle(l, carry):
        store_taps(norm_layer(l, l), x9h.at[l + 1], x9l.at[l + 1], 1)
        return carry

    lax.fori_loop(1, LAYERS - 1, middle, 0)
    act = norm_layer(LAYERS - 1, LAYERS - 1)
    for s in range(SW):
        for i in range(ROWS):
            at = s * PLANE + i * COLS
            features[s, :, i, :] = act[:, at : at + COLS]
            u_ref[:, at : at + COLS] = cot[s, :, i, :]

    def piece(ref, l, i):
        z_at = pl.multiple_of(lax.rem(i, nz) * (C // nz), C // nz)
        l_at = pl.multiple_of((i // nz) * LANES, COLS)
        return ref.at[l, pl.ds(z_at, C // nz), pl.ds(l_at, LANES)]

    def grad_start(l):
        gh = g9h[4 * C : 5 * C, :]
        both = jnp.concatenate([gh, g9l[4 * C : 5 * C, :]], axis=0)
        first = mmt(both, x9h[l])
        dw[l, :, :K9] = first[:C] + first[C:] + mmt(gh, x9l[l])

        def act(i):
            pltpu.make_async_remote_copy(
                src_ref=piece(dw, l, i),
                dst_ref=rs_buf.at[l, me[0]],
                send_sem=g_send.at[l, 0],
                recv_sem=g_recv.at[l, 0],
                device_id=peer(0, i),
                device_id_type=MESH,
            ).start()

        each_peer(0, act)
        rs_buf[l, me[0]] = piece(dw, l, me[0])[...]

    def grad_cross(l):
        settle(0, rs_buf.at[l], g_recv.at[l, 0])
        part = jnp.sum(rs_buf[l], axis=0)
        x_src[l] = part
        x_buf[l, me[1]] = part
        spread(1, x_src.at[l], x_buf.at[l], g_send.at[l, 1], g_recv.at[l, 1])

    def grad_back(l):
        settle(1, x_buf.at[l], g_recv.at[l, 1])
        part = jnp.sum(x_buf[l], axis=0)
        ag_src[l] = part

        def act(i):
            pltpu.make_async_remote_copy(
                src_ref=ag_src.at[l],
                dst_ref=piece(full, l, me[0]),
                send_sem=g_send.at[l, 2],
                recv_sem=g_recv.at[l, 2],
                device_id=peer(0, i),
                device_id_type=MESH,
            ).start()

        each_peer(0, act)
        piece(full, l, me[0])[...] = part

    total_m = 1.0 / (POS * devices)

    def sums_start(l, rnd):
        gy = u_ref[...] * slope[l]
        gy_ref[...] = gy
        send_stat(rnd, 0, to_row(fold(gy), fold(gy * xhat[l])))

    def sums_end(l, rnd):
        send_stat(rnd, 1, jnp.sum(take_stat(rnd, 0), axis=0))
        row = jnp.sum(take_stat(rnd, 1), axis=0)
        norm_out[1, pl.ds(l, 1), :] = row[:, :C]
        norm_out[0, pl.ds(l, 1), :] = pltpu.roll(row, C, 1)[:, :C]
        dy, dx = to_cols(row * total_m)
        n = POS // COLS
        return wide(par[10 + l], n) * (gy_ref[...] - wide(dy, n) - xhat[l] * wide(dx, n))

    def back(t, carry):
        l = LAYERS - 1 - t
        sums_start(l, LAYERS + t)

        @pl.when(t > 0)
        def _():
            grad_start(l + 1)

        @pl.when(t > 1)
        def _():
            grad_cross(l + 2)

        store_taps(sums_end(l, LAYERS + t), g9h, g9l, -1)
        first = mm(wb[l], g9h[...])
        u_ref[...] = first[:C] + first[C:] + mm(wb[l, :C, :], g9l[...])
        return carry

    lax.fori_loop(0, LAYERS - 1, back, 0)
    rnd = 2 * LAYERS - 1
    sums_start(0, rnd)
    grad_start(1)
    grad_cross(2)
    grad_back(3)
    gz = sums_end(0, rnd)
    for b in range(3):
        hi, lo = split(col_shift(gz, 1 if b == 0 else 0))
        for a in range(3):
            at = slice((3 * a + b) * C, (3 * a + b + 1) * C)
            g9h[at, :] = row_shift(hi, 1 if a == 0 else 0)
            g9l[at, :] = row_shift(lo, 1 if a == 0 else 0)
    grad_start(0)
    grad_cross(1)
    grad_back(2)
    u0 = mm(w0h[...], g9h[...]) + mm(w0l[...], g9h[...]) + mm(w0h[...], g9l[...])
    for s in range(SW):
        acc = jnp.zeros((2 * C, PILL), F32)
        for ph in range(4):
            hi, lo = split(u0[ph * C : (ph + 1) * C, s * PLANE : (s + 1) * PLANE])
            both = jnp.concatenate([hi, lo], axis=0)
            acc = acc + mm(both, hot[s, ph * PLANE : (ph + 1) * PLANE, :])
        pillar_out[s] = acc[:C] + acc[C:]
    grad_cross(0)
    grad_back(1)
    grad_back(0)

    for phase in range(2):
        settle(phase, p_buf.at[phase], p_send.at[phase])
        for r in range(2 * LAYERS):
            settle(phase, s_buf.at[r, phase], s_send.at[r, phase])
    for l in range(LAYERS):
        settle(0, rs_buf.at[l], g_send.at[l, 0])
        settle(1, x_buf.at[l], g_send.at[l, 1])
        settle(0, rs_buf.at[l], g_send.at[l, 2])
        settle(0, rs_buf.at[l], g_recv.at[l, 2])
        grads_out[l] = full[l, :, :K9]


def solution(mesh, ny=NY, nz=NZ):
    nx = mesh.shape["rack"] // CORES
    ga, gb = CORES * nz, nx * ny
    gmax = max(ga, gb)
    rows = C // nz

    def per_device(
        points, counts, cells, pfn_w, pfn_g, pfn_b, conv_w, bn_g, bn_b, cotangent
    ):
        taps = conv_w.reshape(LAYERS, 9, C, C)
        w_fwd = taps.transpose(0, 2, 1, 3).reshape(LAYERS, C, K9)
        w_bwd = taps.transpose(0, 3, 1, 2).reshape(LAYERS, C, K9)
        vmem = pl.BlockSpec(memory_space=pltpu.VMEM)
        dma = pltpu.SemaphoreType.DMA
        out = pl.pallas_call(
            functools.partial(step_kernel, (nx, ny, nz)),
            out_shape=(
                jax.ShapeDtypeStruct((SW, C, ROWS, COLS), F32),
                jax.ShapeDtypeStruct((LAYERS, C, K9), F32),
                jax.ShapeDtypeStruct((2, LAYERS, C), F32),
                jax.ShapeDtypeStruct((SW, C, PILL), F32),
            ),
            in_specs=[vmem] * 11,
            out_specs=(vmem,) * 4,
            scratch_shapes=[
                pltpu.VMEM((LAYERS, K9, POS), BF16),
                pltpu.VMEM((LAYERS, K9, POS), BF16),
                pltpu.VMEM((K9, POS), BF16),
                pltpu.VMEM((K9, POS), BF16),
                pltpu.VMEM((SW, 4 * PLANE, PILL), BF16),
                pltpu.VMEM((LAYERS, C, POS), F32),
                pltpu.VMEM((LAYERS, C, POS), F32),
                pltpu.VMEM((LAYERS, 2 * C, K9), BF16),
                pltpu.VMEM((LAYERS, 2 * C, K9), BF16),
                pltpu.VMEM((4 * C, K9), BF16),
                pltpu.VMEM((4 * C, K9), BF16),
                pltpu.VMEM((14, C, COLS), F32),
                pltpu.VMEM((10, C, COLS), F32),
                pltpu.VMEM((SW, C, PILL), F32),
                pltpu.VMEM((SW, C, PILL), F32),
                pltpu.VMEM((C, COLS), F32),
                pltpu.VMEM((C, POS), F32),
                pltpu.VMEM((C, POS), F32),
                pltpu.VMEM((2, 1, 2 * COLS), F32),
                pltpu.VMEM((2, gmax, 1, 2 * COLS), F32),
                pltpu.VMEM((2 * LAYERS, 2, 1, COLS), F32),
                pltpu.VMEM((2 * LAYERS, 2, gmax, 1, COLS), F32),
                pltpu.VMEM((LAYERS, C, 2 * LANES), F32),
                pltpu.VMEM((LAYERS, ga, rows, LANES), F32),
                pltpu.VMEM((LAYERS, rows, LANES), F32),
                pltpu.VMEM((LAYERS, gb, rows, LANES), F32),
                pltpu.VMEM((LAYERS, rows, LANES), F32),
                pltpu.VMEM((LAYERS, C, 2 * LANES), F32),
                dma((2,)),
                dma((2,)),
                dma((2 * LAYERS, 2)),
                dma((2 * LAYERS, 2)),
                dma((LAYERS, 3)),
                dma((LAYERS, 3)),
            ],
            compiler_params=pltpu.CompilerParams(
                collective_id=0, has_side_effects=True, vmem_limit_bytes=60 * 2**20
            ),
        )(
            points,
            counts,
            cells,
            pfn_w,
            pfn_g.reshape(1, C),
            pfn_b.reshape(1, C),
            w_fwd,
            w_bwd,
            bn_g,
            bn_b,
            cotangent,
        )
        features, grads, norm_grads, pillar_grad = out
        grads = grads.reshape(LAYERS, C, 9, C).transpose(0, 2, 1, 3).reshape(LAYERS, 9, C * C)
        return features, grads, norm_grads, pillar_grad

    split_all = ("rack", "chip")
    return jax.shard_map(
        per_device,
        mesh=mesh,
        in_specs=(
            P(split_all, None, None, None),
            P(split_all, None),
            P(split_all, None),
            P(),
            P(),
            P(),
            P(),
            P(),
            P(),
            P(split_all, None, None, None),
        ),
        out_specs=(
            P(split_all, None, None, None),
            P(),
            P(),
            P(split_all, None, None),
        ),
        check_vma=False,
    )
```

profile of v0, /device:TPU:1, one launch (start us, length us, event | category | flops | bytes accessed | tf_op | source)
XLA Modules:
  0.0 139.7 jit_solution(1092365236141499883)
XLA Ops:
  0.6 1.6 %reshape.31 = f32[4,9,64,64]{3,2,0,1:T(8,128)S(1)} reshape(f32[4,9,4096]{2,0,1:T(4,128)} %param.16) | data formatting | bytes 1179648 | tf_op jit(solution)/shard_map/reshape | solution.py:560
  2.3 0.4 copy.22
  2.6 1.2 copy.24.w_fwd
  3.9 0.1 copy.23
  4.0 1.2 copy.25.w_bwd
  5.2 129.3 %shard_map.129 = (f32[2,64,4,128]{3,2,1,0:T(4,128)}, f32[4,64,576]{2,1,0:T(8,128)}, f32[2,4,64]{2,1,0:T(4,128)}, f32[2,64,256]{2,1,0:T(8,128)}) custom-call(f32[2,4,32,256]{3,2,1,0:T(8,128)} %points.1, s32[2,256]{1,0:T(2,128)} %counts.1, s32[2,256]{1,0:T(2,128)} %cells.1, f32[9,64]{1,0:T(8,128)} %pfn_w.1, f32[1,64]{1,0:T(1,128)} %bitcast.20, ...), custom_call_target="tpu_custom_call" | custom-call | tf_op jit(solution)/shard_map/pallas_call | solution.py:565
  134.5 1.5 %copy.26 = f32[4,64,576]{1,2,0:T(8,128)S(1)} copy(f32[4,64,576]{2,1,0:T(8,128)} %get-tuple-element.9) | data formatting | bytes 1179648 | tf_op jit(solution)/shard_map/pallas_call | solution.py:565
  136.0 0.4 copy.27
  136.4 0.0 copy-start
  136.4 0.0 copy-start.2
  136.4 0.0 copy-start.1
  136.4 1.3 reshape.35
  137.7 0.0 copy-done
  137.7 0.7 copy.31
  138.4 0.0 copy-done.2
  138.4 0.6 copy.32
  139.0 0.0 copy-done.1
  139.0 0.7 copy.33
Async XLA Ops:
  136.4 1.3 copy-start
  136.4 2.0 %copy-start.2 = (f32[2,4,64]{2,1,0:T(4,128)S(1)}, f32[2,4,64]{2,1,0:T(4,128)}, u32[]{:S(2)}) copy-start(f32[2,4,64]{2,1,0:T(4,128)} %get-tuple-element.18) | copy-start | bytes 6148
  136.4 2.6 %copy-start.1 = (f32[2,64,256]{2,1,0:T(8,128)S(1)}, f32[2,64,256]{2,1,0:T(8,128)}, u32[]{:S(2)}) copy-start(f32[2,64,256]{2,1,0:T(8,128)} %get-tuple-element.19) | copy-start | bytes 393220
where the time goes:
time: 140 us
  Pallas kernels  129 us (92%)
  local copies, waits for them, and re-layouts  9.67 us (7%)
    pallas_call x1, Pallas kernels, per_device(): pl.pallas_call(functools.partial(step_kernel, (nx, ny, nz)), out_shape=(j...  129 us

commit v1 on v0

--- a/solution.py
+++ b/solution.py
@@ -146,6 +146,13 @@
     x_buf,
     ag_src,
     full,
+    c_src,
+    c_buf,
+    cx_src,
+    cx_buf,
+    trio,
+    c_send,
+    c_recv,
     p_send,
     p_recv,
     s_send,
@@ -154,7 +161,7 @@
     g_recv,
 ):
     nx, ny, nz = size
-    ga, gb = CORES * nz, nx * ny
+    ga, gb = CORES * nx * ny, nz
     devices = ga * gb
     rack = lax.axis_index("rack")
     chip = lax.axis_index("chip")
@@ -162,15 +169,22 @@
     my_x = rack // CORES
     my_z = lax.rem(chip, nz)
     my_y = chip // nz
-    me = (core * nz + my_z, my_x * ny + my_y)
+    mine = my_x * ny + my_y
+    me = (core * (nx * ny) + mine, my_z)
     groups = (ga, gb)
 
     def peer(phase, i):
         if phase == 0:
-            return (my_x * CORES + i // nz, my_y * nz + lax.rem(i, nz))
-        return ((i // ny) * CORES + core, lax.rem(i, ny) * nz + my_z)
-
-    def each_peer(phase, act):
+            at = lax.rem(i, nx * ny)
+            return ((at // ny) * CORES + i // (nx * ny), lax.rem(at, ny) * nz + my_z)
+        return (rack, my_y * nz + i)
+
+    def each_peer(phase, act, unroll=False):
+        if unroll:
+            for d in range(1, groups[phase]):
+                act(lax.rem(me[phase] + d, groups[phase]))
+            return
+
         def one(d, carry):
             act(lax.rem(me[phase] + d, groups[phase]))
             return carry
@@ -186,7 +200,7 @@
             ),
         )
 
-    def spread(phase, src, buf, send, recv):
+    def spread(phase, src, buf, send, recv, unroll=False):
         def act(i):
             pltpu.make_async_remote_copy(
                 src_ref=src,
@@ -197,7 +211,7 @@
                 device_id_type=MESH,
             ).start()
 
-        each_peer(phase, act)
+        each_peer(phase, act, unroll)
 
     def settle(phase, buf, sem):
         part = buf.at[pl.ds(0, groups[phase] - 1)]
@@ -296,7 +310,7 @@
     pl.semaphore_wait(barrier, ga + gb - 2)
     p_src[0] = payload
     p_buf[0, me[0]] = payload
-    spread(0, p_src.at[0], p_buf.at[0], p_send.at[0], p_recv.at[0])
+    spread(0, p_src.at[0], p_buf.at[0], p_send.at[0], p_recv.at[0], True)
 
     for s in range(SW):
         cell = cells[s : s + 1, :]
@@ -328,14 +342,12 @@
         hi, lo = split(jnp.where(parity == ph, w_bwd[0], 0.0))
         w0h[ph * C : (ph + 1) * C, :] = hi
         w0l[ph * C : (ph + 1) * C, :] = lo
-    for l in range(LAYERS):
-        dw[l, :, K9:] = jnp.zeros((C, 2 * LANES - K9), F32)
 
     settle(0, p_buf.at[0], p_recv.at[0])
     payload = merge_pfn(p_buf[0, pl.ds(0, ga)])
     p_src[1] = payload
     p_buf[1, me[1]] = payload
-    spread(1, p_src.at[1], p_buf.at[1], p_send.at[1], p_recv.at[1])
+    spread(1, p_src.at[1], p_buf.at[1], p_send.at[1], p_recv.at[1], True)
     settle(1, p_buf.at[1], p_recv.at[1])
     payload = merge_pfn(p_buf[1, pl.ds(0, gb)])
     row, total = payload[:, :COLS], payload[:, COLS:]
@@ -374,6 +386,7 @@
             s_buf.at[rnd, phase],
             s_send.at[rnd, phase],
             s_recv.at[rnd, phase],
+            True,
         )
 
     def take_stat(rnd, phase):
@@ -387,7 +400,7 @@
         spread_sq = jnp.sum(dev * dev, axis=0) * count
         return jnp.where(low, avg, total + pltpu.roll(spread_sq, C, 1))
 
-    def norm_layer(l, rnd):
+    def norm_layer(l, rnd, meanwhile=None):
         xh = x9h.at[l]
         xl = x9l.at[l]
         wide_z = mm(wf[l], xh[...])
@@ -397,6 +410,8 @@
         dev = z - m
         row = to_row(part, fold(dev * dev))
         send_stat(rnd, 0, jnp.where(low, row * (1.0 / POS), row))
+        if meanwhile is not None:
+            meanwhile()
         row = merge_norm(take_stat(rnd, 0), float(POS))
         send_stat(rnd, 1, row)
         row = merge_norm(take_stat(rnd, 1), float(POS * ga))
@@ -412,10 +427,58 @@
         par[10 + l] = gain * inv_col
         return act
 
+    rows = C // (nx * ny)
+    pad = jnp.zeros((C, 2 * LANES - K9), F32)
+
+    def pieces(value):
+        value = jnp.concatenate([value, pad], axis=1)
+        for i in range(ga):
+            r_at = (i % (nx * ny)) * rows
+            l_at = (i // (nx * ny)) * LANES
+            yield i, value[r_at : r_at + rows, l_at : l_at + LANES]
+
+    def scatter(src, buf, send, recv):
+        def act(i):
+            pltpu.make_async_remote_copy(
+                src_ref=src.at[i],
+                dst_ref=buf.at[me[0]],
+                send_sem=send,
+                recv_sem=recv,
+                device_id=peer(0, i),
+                device_id_type=MESH,
+            ).start()
+
+        each_peer(0, act)
+        buf[me[0]] = src[me[0]]
+
+    def fixed_start():
+        hi, lo = split(xhat[0])
+        ones = jnp.ones((C, POS), BF16)
+        first = mmt(jnp.concatenate([hi, lo, ones], axis=0), x9h[0])
+        second = mmt(jnp.concatenate([hi, ones], axis=0), x9l[0])
+        corr = first[:C] + first[C : 2 * C] + second[:C]
+        plain = first[2 * C : 3 * C] + second[C : 2 * C]
+        for i, part in pieces(corr):
+            c_src[i, :rows, :] = part
+        for i, part in pieces(plain):
+            c_src[i, rows:, :] = part
+        scatter(c_src, c_buf, c_send.at[0], c_recv.at[0])
+
+    def fixed_cross():
+        settle(0, c_buf, c_recv.at[0])
+        part = jnp.sum(c_buf[...], axis=0)
+        cx_src[...] = part
+        cx_buf[me[1]] = part
+        spread(1, cx_src, cx_buf, c_send.at[1], c_recv.at[1])
+
     store_taps(norm_layer(0, 0), x9h.at[1], x9l.at[1], 1)
 
     def middle(l, carry):
-        store_taps(norm_layer(l, l), x9h.at[l + 1], x9l.at[l + 1], 1)
+        def meanwhile():
+            pl.when(l == 1)(fixed_start)
+            pl.when(l == 2)(fixed_cross)
+
+        store_taps(norm_layer(l, l, meanwhile), x9h.at[l + 1], x9l.at[l + 1], 1)
         return carry
 
     lax.fori_loop(1, LAYERS - 1, middle, 0)
@@ -426,29 +489,14 @@
             features[s, :, i, :] = act[:, at : at + COLS]
             u_ref[:, at : at + COLS] = cot[s, :, i, :]
 
-    def piece(ref, l, i):
-        z_at = pl.multiple_of(lax.rem(i, nz) * (C // nz), C // nz)
-        l_at = pl.multiple_of((i // nz) * LANES, COLS)
-        return ref.at[l, pl.ds(z_at, C // nz), pl.ds(l_at, LANES)]
-
-    def grad_start(l):
-        gh = g9h[4 * C : 5 * C, :]
-        both = jnp.concatenate([gh, g9l[4 * C : 5 * C, :]], axis=0)
+    def grad_start(l, gh=None, gl=None):
+        if gh is None:
+            gh, gl = g9h[4 * C : 5 * C, :], g9l[4 * C : 5 * C, :]
+        both = jnp.concatenate([gh, gl], axis=0)
         first = mmt(both, x9h[l])
-        dw[l, :, :K9] = first[:C] + first[C:] + mmt(gh, x9l[l])
-
-        def act(i):
-            pltpu.make_async_remote_copy(
-                src_ref=piece(dw, l, i),
-                dst_ref=rs_buf.at[l, me[0]],
-                send_sem=g_send.at[l, 0],
-                recv_sem=g_recv.at[l, 0],
-                device_id=peer(0, i),
-                device_id_type=MESH,
-            ).start()
-
-        each_peer(0, act)
-        rs_buf[l, me[0]] = piece(dw, l, me[0])[...]
+        for i, part in pieces(first[:C] + first[C:] + mmt(gh, x9l[l])):
+            dw[l, i] = part
+        scatter(dw.at[l], rs_buf.at[l], g_send.at[l, 0], g_recv.at[l, 0])
 
     def grad_cross(l):
         settle(0, rs_buf.at[l], g_recv.at[l, 0])
@@ -457,23 +505,15 @@
         x_buf[l, me[1]] = part
         spread(1, x_src.at[l], x_buf.at[l], g_send.at[l, 1], g_recv.at[l, 1])
 
-    def grad_back(l):
+    def grad_back(l, finish=None):
         settle(1, x_buf.at[l], g_recv.at[l, 1])
         part = jnp.sum(x_buf[l], axis=0)
+        if finish is not None:
+            part = finish(part)
         ag_src[l] = part
 
-        def act(i):
-            pltpu.make_async_remote_copy(
-                src_ref=ag_src.at[l],
-                dst_ref=piece(full, l, me[0]),
-                send_sem=g_send.at[l, 2],
-                recv_sem=g_recv.at[l, 2],
-                device_id=peer(0, i),
-                device_id_type=MESH,
-            ).start()
-
-        each_peer(0, act)
-        piece(full, l, me[0])[...] = part
+        spread(0, ag_src.at[l], full.at[l], g_send.at[l, 2], g_recv.at[l, 2])
+        full[l, me[0]] = part
 
     total_m = 1.0 / (POS * devices)
 
@@ -482,12 +522,16 @@
         gy_ref[...] = gy
         send_stat(rnd, 0, to_row(fold(gy), fold(gy * xhat[l])))
 
+    def sums_cross(rnd):
+        send_stat(rnd, 1, jnp.sum(take_stat(rnd, 0), axis=0))
+
     def sums_end(l, rnd):
-        send_stat(rnd, 1, jnp.sum(take_stat(rnd, 0), axis=0))
         row = jnp.sum(take_stat(rnd, 1), axis=0)
         norm_out[1, pl.ds(l, 1), :] = row[:, :C]
         norm_out[0, pl.ds(l, 1), :] = pltpu.roll(row, C, 1)[:, :C]
-        dy, dx = to_cols(row * total_m)
+        return to_cols(row * total_m)
+
+    def grad_z(l, dy, dx):
         n = POS // COLS
         return wide(par[10 + l], n) * (gy_ref[...] - wide(dy, n) - xhat[l] * wide(dx, n))
 
@@ -501,9 +545,15 @@
 
         @pl.when(t > 1)
         def _():
-            grad_cross(l + 2)
-
-        store_taps(sums_end(l, LAYERS + t), g9h, g9l, -1)
+            grad_back(l + 2)
+
+        sums_cross(LAYERS + t)
+
+        @pl.when(t > 0)
+        def _():
+            grad_cross(l + 1)
+
+        store_taps(grad_z(l, *sums_end(l, LAYERS + t)), g9h, g9l, -1)
         first = mm(wb[l], g9h[...])
         u_ref[...] = first[:C] + first[C:] + mm(wb[l, :C, :], g9l[...])
         return carry
@@ -511,19 +561,32 @@
     lax.fori_loop(0, LAYERS - 1, back, 0)
     rnd = 2 * LAYERS - 1
     sums_start(0, rnd)
+    grad_start(0, *split(gy_ref[...]))
     grad_start(1)
-    grad_cross(2)
-    grad_back(3)
-    gz = sums_end(0, rnd)
+    grad_back(2)
+    sums_cross(rnd)
+    grad_cross(0)
+    grad_cross(1)
+    settle(1, cx_buf, c_recv.at[1])
+    fixed = jnp.sum(cx_buf[...], axis=0)
+    dy, dx = sums_end(0, rnd)
+    for k, tile in enumerate((dy, dx, par[10])):
+        for q in range(nx * ny):
+            trio[k, q] = tile[q * rows : (q + 1) * rows]
+
+    def finish(part):
+        dy_m, dx_m, k_m = [wide(trio[k, mine], LANES // COLS) for k in range(3)]
+        return k_m * (part - fixed[rows:] * dy_m - fixed[:rows] * dx_m)
+
+    grad_back(0, finish)
+    grad_back(1)
+    gz = grad_z(0, dy, dx)
     for b in range(3):
         hi, lo = split(col_shift(gz, 1 if b == 0 else 0))
         for a in range(3):
             at = slice((3 * a + b) * C, (3 * a + b + 1) * C)
             g9h[at, :] = row_shift(hi, 1 if a == 0 else 0)
             g9l[at, :] = row_shift(lo, 1 if a == 0 else 0)
-    grad_start(0)
-    grad_cross(1)
-    grad_back(2)
     u0 = mm(w0h[...], g9h[...]) + mm(w0l[...], g9h[...]) + mm(w0h[...], g9l[...])
     for s in range(SW):
         acc = jnp.zeros((2 * C, PILL), F32)
@@ -532,27 +595,30 @@
             both = jnp.concatenate([hi, lo], axis=0)
             acc = acc + mm(both, hot[s, ph * PLANE : (ph + 1) * PLANE, :])
         pillar_out[s] = acc[:C] + acc[C:]
-    grad_cross(0)
-    grad_back(1)
-    grad_back(0)
 
     for phase in range(2):
         settle(phase, p_buf.at[phase], p_send.at[phase])
         for r in range(2 * LAYERS):
             settle(phase, s_buf.at[r, phase], s_send.at[r, phase])
+    settle(0, c_buf, c_send.at[0])
+    settle(1, cx_buf, c_send.at[1])
     for l in range(LAYERS):
         settle(0, rs_buf.at[l], g_send.at[l, 0])
         settle(1, x_buf.at[l], g_send.at[l, 1])
         settle(0, rs_buf.at[l], g_send.at[l, 2])
         settle(0, rs_buf.at[l], g_recv.at[l, 2])
-        grads_out[l] = full[l, :, :K9]
+        for i in range(ga):
+            r_at = (i % (nx * ny)) * rows
+            l_at = (i // (nx * ny)) * LANES
+            width = min(LANES, K9 - l_at)
+            grads_out[l, r_at : r_at + rows, l_at : l_at + width] = full[l, i, :, :width]
 
 
 def solution(mesh, ny=NY, nz=NZ):
     nx = mesh.shape["rack"] // CORES
-    ga, gb = CORES * nz, nx * ny
+    ga, gb = CORES * nx * ny, nz
     gmax = max(ga, gb)
-    rows = C // nz
+    rows = C // (nx * ny)
 
     def per_device(
         points, counts, cells, pfn_w, pfn_g, pfn_b, conv_w, bn_g, bn_b, cotangent
@@ -595,12 +661,19 @@
                 pltpu.VMEM((2, gmax, 1, 2 * COLS), F32),
                 pltpu.VMEM((2 * LAYERS, 2, 1, COLS), F32),
                 pltpu.VMEM((2 * LAYERS, 2, gmax, 1, COLS), F32),
-                pltpu.VMEM((LAYERS, C, 2 * LANES), F32),
+                pltpu.VMEM((LAYERS, ga, rows, LANES), F32),
                 pltpu.VMEM((LAYERS, ga, rows, LANES), F32),
                 pltpu.VMEM((LAYERS, rows, LANES), F32),
                 pltpu.VMEM((LAYERS, gb, rows, LANES), F32),
                 pltpu.VMEM((LAYERS, rows, LANES), F32),
-                pltpu.VMEM((LAYERS, C, 2 * LANES), F32),
+                pltpu.VMEM((LAYERS, ga, rows, LANES), F32),
+                pltpu.VMEM((ga, 2 * rows, LANES), F32),
+                pltpu.VMEM((ga, 2 * rows, LANES), F32),
+                pltpu.VMEM((2 * rows, LANES), F32),
+                pltpu.VMEM((gb, 2 * rows, LANES), F32),
+                pltpu.VMEM((3, ga // CORES, rows, COLS), F32),
+                dma((2,)),
+                dma((2,)),
                 dma((2,)),
                 dma((2,)),
                 dma((2 * LAYERS, 2)),

time: 140 us -> 127 us (0.907)
  Pallas kernels: 129 us -> 116 us
    pallas_call x1, Pallas kernels: 129 us -> 116 us  [per_device(): pl.pallas_call(functools.partial(step_kernel, (nx, ny, nz)), out_shape=(j...]
where the time goes in v1:
time: 127 us
  Pallas kernels  116 us (91%)
  local copies, waits for them, and re-layouts  9.67 us (8%)
    pallas_call x1, Pallas kernels, per_device(): pl.pallas_call(functools.partial(step_kernel, (nx, ny, nz)), out_shape=(j...  116 us

profile of v1, /device:TPU:1, one launch (start us, length us, event | category | flops | bytes accessed | tf_op | source)
XLA Modules:
  0.0 126.8 jit_solution(16054507464826503122)
XLA Ops:
  0.6 1.6 %reshape.31 = f32[4,9,64,64]{3,2,0,1:T(8,128)S(1)} reshape(f32[4,9,4096]{2,0,1:T(4,128)} %param.16) | data formatting | bytes 1179648 | tf_op jit(solution)/shard_map/reshape | solution.py:626
  2.3 0.4 copy.22
  2.6 1.2 copy.24.w_fwd
  3.9 0.1 copy.23
  4.0 1.2 copy.25.w_bwd
  5.2 116.4 %shard_map.129 = (f32[2,64,4,128]{3,2,1,0:T(4,128)}, f32[4,64,576]{2,1,0:T(8,128)}, f32[2,4,64]{2,1,0:T(4,128)}, f32[2,64,256]{2,1,0:T(8,128)}) custom-call(f32[2,4,32,256]{3,2,1,0:T(8,128)} %points.1, s32[2,256]{1,0:T(2,128)} %counts.1, s32[2,256]{1,0:T(2,128)} %cells.1, f32[9,64]{1,0:T(8,128)} %pfn_w.1, f32[1,64]{1,0:T(1,128)} %bitcast.20, ...), custom_call_target="tpu_custom_call" | custom-call | tf_op jit(solution)/shard_map/pallas_call | solution.py:631
  121.6 1.5 %copy.26 = f32[4,64,576]{1,2,0:T(8,128)S(1)} copy(f32[4,64,576]{2,1,0:T(8,128)} %get-tuple-element.9) | data formatting | bytes 1179648 | tf_op jit(solution)/shard_map/pallas_call | solution.py:631
  123.1 0.4 copy.27
  123.5 0.0 copy-start
  123.5 0.0 copy-start.2
  123.5 0.0 copy-start.1
  123.5 1.3 %reshape.35 = f32[4,9,4096]{2,0,1:T(4,128)} reshape(f32[4,9,64,64]{3,2,0,1:T(8,128)S(1)} %copy.27) | data formatting | bytes 1179648 | tf_op jit(solution)/shard_map/reshape | solution.py:701
  124.8 0.0 copy-done
  124.8 0.7 copy.31
  125.5 0.0 copy-done.2
  125.5 0.6 copy.32
  126.1 0.0 copy-done.1
  126.1 0.7 copy.33
Async XLA Ops:
  123.5 1.3 %copy-start = (f32[2,64,4,128]{3,2,1,0:T(4,128)S(1)}, f32[2,64,4,128]{3,2,1,0:T(4,128)}, u32[]{:S(2)}) copy-start(f32[2,64,4,128]{3,2,1,0:T(4,128)} %get-tuple-element.16) | copy-start | bytes 786436
  123.5 2.0 %copy-start.2 = (f32[2,4,64]{2,1,0:T(4,128)S(1)}, f32[2,4,64]{2,1,0:T(4,128)}, u32[]{:S(2)}) copy-start(f32[2,4,64]{2,1,0:T(4,128)} %get-tuple-element.18) | copy-start | bytes 6148
  123.5 2.6 %copy-start.1 = (f32[2,64,256]{2,1,0:T(8,128)S(1)}, f32[2,64,256]{2,1,0:T(8,128)}, u32[]{:S(2)}) copy-start(f32[2,64,256]{2,1,0:T(8,128)} %get-tuple-element.19) | copy-start | bytes 393220

commit v2 on v1

--- a/solution.py
+++ b/solution.py
@@ -22,6 +22,7 @@
 NZ = 8
 NY = 4
 LANES = 384
+VLIM = 60
 MESH = pl.DeviceIdType.MESH
 F32 = jnp.float32
 BF16 = jnp.bfloat16
@@ -109,8 +110,7 @@
     pfn_w,
     pfn_g,
     pfn_b,
-    w_fwd,
-    w_bwd,
+    conv_w,
     bn_g,
     bn_b,
     cot,
@@ -129,6 +129,7 @@
     wb,
     w0h,
     w0l,
+    w_raw,
     par,
     pwc,
     hmax,
@@ -330,24 +331,60 @@
     for l in range(LAYERS):
         par[2 + 2 * l], par[3 + 2 * l] = columns(bn_g[l : l + 1, :], bn_b[l : l + 1, :])
 
-    def load_weights(l, carry):
-        wf[l, :C, :], wf[l, C:, :] = split(w_fwd[l])
-        wb[l, :C, :], wb[l, C:, :] = split(w_bwd[l])
+    pairs = 5
+
+    def spread_rows(block, carry):
+        for step in range(8):
+            t = block * 8 + step
+            at = pl.ds(pl.multiple_of(t * COLS, COLS), COLS)
+            for k in range(pairs):
+                a = conv_w[2 * k, :, at]
+                b = conv_w[min(2 * k + 1, 8), :, at]
+                w_raw[2 * t, k] = jnp.where(low, a, pltpu.roll(b, C, 1))
+                w_raw[2 * t + 1, k] = jnp.where(low, pltpu.roll(a, C, 1), b)
         return carry
 
-    lax.fori_loop(0, LAYERS, load_weights, 0)
-    tap = lax.broadcasted_iota(jnp.int32, (C, K9), 1) // C
-    parity = jnp.where(tap // 3 == 1, 0, 2) + jnp.where(lax.rem(tap, 3) == 1, 0, 1)
-    for ph in range(4):
-        hi, lo = split(jnp.where(parity == ph, w_bwd[0], 0.0))
-        w0h[ph * C : (ph + 1) * C, :] = hi
-        w0l[ph * C : (ph + 1) * C, :] = lo
+    lax.fori_loop(0, C // 16, spread_rows, 0)
+
+    def taps_of(l, k):
+        return w_raw[:, k, l, :]
+
+    def turned(l, k):
+        tile = taps_of(l, k).T
+        return jnp.concatenate([tile[:C], tile[C:]], axis=1)
+
+    def pair_lanes(k):
+        return slice(k * COLS, min((k + 1) * COLS, K9))
+
+    def forward_weights(l):
+        for k in range(pairs):
+            lanes = pair_lanes(k)
+            tile = taps_of(l, k)[:, : lanes.stop - lanes.start]
+            wf[l, :C, lanes], wf[l, C:, lanes] = split(tile)
+
+    def backward_weights():
+        for l in range(1, LAYERS):
+            for k in range(pairs):
+                lanes = pair_lanes(k)
+                tile = turned(l, k)[:, : lanes.stop - lanes.start]
+                wb[l, :C, lanes], wb[l, C:, lanes] = split(tile)
+        w_bwd0 = jnp.concatenate([turned(0, k) for k in range(pairs)], axis=1)[:, :K9]
+        tap = lax.broadcasted_iota(jnp.int32, (C, K9), 1) // C
+        parity = jnp.where(tap // 3 == 1, 0, 2) + jnp.where(lax.rem(tap, 3) == 1, 0, 1)
+        for ph in range(4):
+            hi, lo = split(jnp.where(parity == ph, w_bwd0, 0.0))
+            w0h[ph * C : (ph + 1) * C, :] = hi
+            w0l[ph * C : (ph + 1) * C, :] = lo
+
+    forward_weights(0)
 
     settle(0, p_buf.at[0], p_recv.at[0])
     payload = merge_pfn(p_buf[0, pl.ds(0, ga)])
     p_src[1] = payload
     p_buf[1, me[1]] = payload
     spread(1, p_src.at[1], p_buf.at[1], p_send.at[1], p_recv.at[1], True)
+    for l in range(1, LAYERS):
+        forward_weights(l)
     settle(1, p_buf.at[1], p_recv.at[1])
     payload = merge_pfn(p_buf[1, pl.ds(0, gb)])
     row, total = payload[:, :COLS], payload[:, COLS:]
@@ -471,7 +508,7 @@
         cx_buf[me[1]] = part
         spread(1, cx_src, cx_buf, c_send.at[1], c_recv.at[1])
 
-    store_taps(norm_layer(0, 0), x9h.at[1], x9l.at[1], 1)
+    store_taps(norm_layer(0, 0, backward_weights), x9h.at[1], x9l.at[1], 1)
 
     def middle(l, carry):
         def meanwhile():
@@ -510,10 +547,18 @@
         part = jnp.sum(x_buf[l], axis=0)
         if finish is not None:
             part = finish(part)
-        ag_src[l] = part
-
+        for k in range(LANES // COLS):
+            tile = part[:, k * COLS : (k + 1) * COLS]
+            swapped = pltpu.roll(tile, C, 1)
+            for p in range(rows // 2):
+                even, odd = slice(2 * p, 2 * p + 1), slice(2 * p + 1, 2 * p + 2)
+                lanes = slice(p * COLS, (p + 1) * COLS)
+                first = jnp.where(low, tile[even], swapped[odd])
+                second = jnp.where(low, swapped[even], tile[odd])
+                ag_src[l, 2 * k : 2 * k + 1, lanes] = first
+                ag_src[l, 2 * k + 1 : 2 * k + 2, lanes] = second
         spread(0, ag_src.at[l], full.at[l], g_send.at[l, 2], g_recv.at[l, 2])
-        full[l, me[0]] = part
+        full[l, me[0]] = ag_src[l]
 
     total_m = 1.0 / (POS * devices)
 
@@ -605,13 +650,37 @@
     for l in range(LAYERS):
         settle(0, rs_buf.at[l], g_send.at[l, 0])
         settle(1, x_buf.at[l], g_send.at[l, 1])
-        settle(0, rs_buf.at[l], g_send.at[l, 2])
-        settle(0, rs_buf.at[l], g_recv.at[l, 2])
+        settle(0, full.at[l], g_send.at[l, 2])
+        settle(0, full.at[l], g_recv.at[l, 2])
+        span = rows * C
         for i in range(ga):
-            r_at = (i % (nx * ny)) * rows
-            l_at = (i // (nx * ny)) * LANES
-            width = min(LANES, K9 - l_at)
-            grads_out[l, r_at : r_at + rows, l_at : l_at + width] = full[l, i, :, :width]
+            lanes = slice((i % (nx * ny)) * span, (i % (nx * ny) + 1) * span)
+            first = (i // (nx * ny)) * (LANES // C)
+            count = min(LANES // C, 9 - first)
+            grads_out[first : first + count, l, lanes] = full[l, i, :count, :]
+
+
+def deliver_kernel(*refs):
+    *refs, sem = refs
+    half = len(refs) // 2
+    copies = [
+        pltpu.make_async_copy(refs[k], refs[half + k], sem.at[k]) for k in range(half)
+    ]
+    for copy in copies:
+        copy.start()
+    for copy in copies:
+        copy.wait()
+
+
+def deliver(arrays):
+    return pl.pallas_call(
+        deliver_kernel,
+        out_shape=tuple(jax.ShapeDtypeStruct(a.shape, a.dtype) for a in arrays),
+        in_specs=[pl.BlockSpec(memory_space=pltpu.VMEM)] * len(arrays),
+        out_specs=(pl.BlockSpec(memory_space=pl.ANY),) * len(arrays),
+        scratch_shapes=[pltpu.SemaphoreType.DMA((len(arrays),))],
+        compiler_params=pltpu.CompilerParams(vmem_limit_bytes=VLIM * 2**20),
+    )(*arrays)
 
 
 def solution(mesh, ny=NY, nz=NZ):
@@ -623,20 +692,17 @@
     def per_device(
         points, counts, cells, pfn_w, pfn_g, pfn_b, conv_w, bn_g, bn_b, cotangent
     ):
-        taps = conv_w.reshape(LAYERS, 9, C, C)
-        w_fwd = taps.transpose(0, 2, 1, 3).reshape(LAYERS, C, K9)
-        w_bwd = taps.transpose(0, 3, 1, 2).reshape(LAYERS, C, K9)
         vmem = pl.BlockSpec(memory_space=pltpu.VMEM)
         dma = pltpu.SemaphoreType.DMA
         out = pl.pallas_call(
             functools.partial(step_kernel, (nx, ny, nz)),
             out_shape=(
                 jax.ShapeDtypeStruct((SW, C, ROWS, COLS), F32),
-                jax.ShapeDtypeStruct((LAYERS, C, K9), F32),
+                jax.ShapeDtypeStruct((9, LAYERS, C * C), F32),
                 jax.ShapeDtypeStruct((2, LAYERS, C), F32),
                 jax.ShapeDtypeStruct((SW, C, PILL), F32),
             ),
-            in_specs=[vmem] * 11,
+            in_specs=[vmem] * 10,
             out_specs=(vmem,) * 4,
             scratch_shapes=[
                 pltpu.VMEM((LAYERS, K9, POS), BF16),
@@ -650,6 +716,7 @@
                 pltpu.VMEM((LAYERS, 2 * C, K9), BF16),
                 pltpu.VMEM((4 * C, K9), BF16),
                 pltpu.VMEM((4 * C, K9), BF16),
+                pltpu.VMEM((C, 5, LAYERS, COLS), F32),
                 pltpu.VMEM((14, C, COLS), F32),
                 pltpu.VMEM((10, C, COLS), F32),
                 pltpu.VMEM((SW, C, PILL), F32),
@@ -665,8 +732,8 @@
                 pltpu.VMEM((LAYERS, ga, rows, LANES), F32),
                 pltpu.VMEM((LAYERS, rows, LANES), F32),
                 pltpu.VMEM((LAYERS, gb, rows, LANES), F32),
-                pltpu.VMEM((LAYERS, rows, LANES), F32),
-                pltpu.VMEM((LAYERS, ga, rows, LANES), F32),
+                pltpu.VMEM((LAYERS, LANES // C, rows * C), F32),
+                pltpu.VMEM((LAYERS, ga, LANES // C, rows * C), F32),
                 pltpu.VMEM((ga, 2 * rows, LANES), F32),
                 pltpu.VMEM((ga, 2 * rows, LANES), F32),
                 pltpu.VMEM((2 * rows, LANES), F32),
@@ -682,7 +749,7 @@
                 dma((LAYERS, 3)),
             ],
             compiler_params=pltpu.CompilerParams(
-                collective_id=0, has_side_effects=True, vmem_limit_bytes=60 * 2**20
+                collective_id=0, has_side_effects=True, vmem_limit_bytes=VLIM * 2**20
             ),
         )(
             points,
@@ -691,15 +758,13 @@
             pfn_w,
             pfn_g.reshape(1, C),
             pfn_b.reshape(1, C),
-            w_fwd,
-            w_bwd,
+            conv_w.transpose(1, 0, 2),
             bn_g,
             bn_b,
             cotangent,
         )
-        features, grads, norm_grads, pillar_grad = out
-        grads = grads.reshape(LAYERS, C, 9, C).transpose(0, 2, 1, 3).reshape(LAYERS, 9, C * C)
-        return features, grads, norm_grads, pillar_grad
+        features, grads, norm_grads, pillar_grad = deliver(out)
+        return features, grads.transpose(1, 0, 2), norm_grads, pillar_grad
 
     split_all = ("rack", "chip")
     return jax.shard_map(

time: 127 us -> 121 us (0.953)
  local copies, waits for them, and re-layouts: 9.67 us -> 0 us
  Pallas kernels: 116 us -> 120 us
    reshape x6 -> x0, local copies, waits for them, and re-layouts: 5.89 us -> none  [the longest x3 2.12 us: per_device(): taps = conv_w.reshape(LAYERS, 9, C, C)]
    pallas_call x0 -> x1, Pallas kernels: none -> 2.14 us  [deliver(): pl.pallas_call(deliver_kernel, out_shape=tuple((jax.ShapeDtypeStruct(a.sh...]
    unnamed x9 -> x0, local copies, waits for them, and re-layouts: 1.96 us -> none
    pallas_call x1, Pallas kernels: 116 us -> 118 us  [per_device(): pl.pallas_call(functools.partial(step_kernel, (nx, ny, nz)), out_shape=(j...]
    pallas_call x1 -> x0, local copies, waits for them, and re-layouts: 1.45 us -> none  [per_device(): pl.pallas_call(functools.partial(step_kernel, (nx, ny, nz)), out_shape=(j...]
where the time goes in v2:
time: 121 us
  Pallas kernels  120 us (99%)
    pallas_call x1, Pallas kernels, per_device(): pl.pallas_call(functools.partial(step_kernel, (nx, ny, nz)), out_shape=(j...  118 us

profile of v2, /device:TPU:1, one launch (start us, length us, event | category | flops | bytes accessed | tf_op | source)
XLA Modules:
  0.0 120.7 jit_solution(5813220326900513640)
XLA Ops:
  0.6 117.9 %shard_map.129 = (f32[2,64,4,128]{3,2,1,0:T(4,128)}, f32[9,4,4096]{2,1,0:T(4,128)}, f32[2,4,64]{2,1,0:T(4,128)}, f32[2,64,256]{2,1,0:T(8,128)}) custom-call(f32[2,4,32,256]{3,2,1,0:T(8,128)} %points.1, s32[2,256]{1,0:T(2,128)} %counts.1, s32[2,256]{1,0:T(2,128)} %cells.1, f32[9,64]{1,0:T(8,128)} %pfn_w.1, f32[1,64]{1,0:T(1,128)} %bitcast.5, ...), custom_call_target="tpu_custom_call" | custom-call | tf_op jit(solution)/shard_map/pallas_call | solution.py:697
  118.5 2.1 %shard_map.130 = (f32[2,64,4,128]{3,2,1,0:T(4,128)}, f32[9,4,4096]{2,1,0:T(4,128)}, f32[2,4,64]{2,1,0:T(4,128)}, f32[2,64,256]{2,1,0:T(8,128)}) custom-call(f32[2,64,4,128]{3,2,1,0:T(4,128)} %get-tuple-element.12.refs_0_, f32[9,4,4096]{2,1,0:T(4,128)} %get-tuple-element.13.refs_1_, f32[2,4,64]{2,1,0:T(4,128)} %get-tuple-element.14.refs_2_, ...), custom_call_target="tpu_custom_call" | custom-call | tf_op jit(solution)/shard_map/pallas_call | solution.py:676

commit v3 on v2

--- a/solution.py
+++ b/solution.py
@@ -152,8 +152,22 @@
     cx_src,
     cx_buf,
     trio,
+    zh,
+    zl,
+    d_src,
+    d_buf,
+    dx_src,
+    dx_buf,
+    dg_src,
+    d_full,
+    q_src,
+    q_buf,
     c_send,
     c_recv,
+    d_send,
+    d_recv,
+    q_send,
+    q_recv,
     p_send,
     p_recv,
     s_send,
@@ -437,7 +451,7 @@
         spread_sq = jnp.sum(dev * dev, axis=0) * count
         return jnp.where(low, avg, total + pltpu.roll(spread_sq, C, 1))
 
-    def norm_layer(l, rnd, meanwhile=None):
+    def norm_layer(l, rnd, meanwhile=None, later=None):
         xh = x9h.at[l]
         xl = x9l.at[l]
         wide_z = mm(wf[l], xh[...])
@@ -451,6 +465,8 @@
             meanwhile()
         row = merge_norm(take_stat(rnd, 0), float(POS))
         send_stat(rnd, 1, row)
+        if later is not None:
+            later()
         row = merge_norm(take_stat(rnd, 1), float(POS * ga))
         mean_col, inv_col = to_cols(
             jnp.where(low, row, lax.rsqrt(row * (1.0 / (POS * devices)) + EPS))
@@ -519,7 +535,48 @@
         return carry
 
     lax.fori_loop(1, LAYERS - 1, middle, 0)
-    act = norm_layer(LAYERS - 1, LAYERS - 1)
+    part_d = 2 * C // ga
+
+    def pair_start():
+        q = jnp.concatenate([slope[1], slope[1] * xhat[1]], axis=0)
+        qh, ql = split(q)
+        both = jnp.concatenate([qh, ql], axis=0)
+        weight = wb[2, :C, :].astype(F32) + wb[2, C:, :].astype(F32)
+        weight = jnp.concatenate([weight, weight], axis=0)
+
+        def per_channel(e):
+            p = e * weight
+            t = p[:, :COLS]
+            for k in range(1, 4):
+                t = t + p[:, k * COLS : (k + 1) * COLS]
+            return t[:, :C] + t[:, C:] + p[:, 4 * COLS :]
+
+        store_taps(xhat[2], g9h, g9l, -1)
+        e = mmt(both, g9h[...])
+        by_normed = per_channel(e[: 2 * C] + e[2 * C :] + mmt(qh, g9l[...]))
+        store_taps(jnp.ones((C, POS), F32), g9h, g9l, -1)
+        e = mmt(both, g9h[...])
+        by_one = per_channel(e[: 2 * C] + e[2 * C :])
+        factors = jnp.concatenate([by_one, by_normed], axis=1).T
+        for i in range(ga):
+            d_src[i] = factors[i * part_d : (i + 1) * part_d]
+        scatter(d_src, d_buf, d_send.at[0], d_recv.at[0])
+
+    def pair_cross():
+        settle(0, d_buf, d_recv.at[0])
+        part = jnp.sum(d_buf[...], axis=0)
+        dx_src[...] = part
+        dx_buf[me[1]] = part
+        spread(1, dx_src, dx_buf, d_send.at[1], d_recv.at[1])
+
+    def pair_back():
+        settle(1, dx_buf, d_recv.at[1])
+        part = jnp.sum(dx_buf[...], axis=0)
+        dg_src[...] = part
+        spread(0, dg_src, d_full, d_send.at[2], d_recv.at[2])
+        d_full[me[0]] = part
+
+    act = norm_layer(LAYERS - 1, LAYERS - 1, pair_start, pair_cross)
     for s in range(SW):
         for i in range(ROWS):
             at = s * PLANE + i * COLS
@@ -528,7 +585,7 @@
 
     def grad_start(l, gh=None, gl=None):
         if gh is None:
-            gh, gl = g9h[4 * C : 5 * C, :], g9l[4 * C : 5 * C, :]
+            gh, gl = zh[l], zl[l]
         both = jnp.concatenate([gh, gl], axis=0)
         first = mmt(both, x9h[l])
         for i, part in pieces(first[:C] + first[C:] + mmt(gh, x9l[l])):
@@ -571,46 +628,63 @@
         send_stat(rnd, 1, jnp.sum(take_stat(rnd, 0), axis=0))
 
     def sums_end(l, rnd):
-        row = jnp.sum(take_stat(rnd, 1), axis=0)
-        norm_out[1, pl.ds(l, 1), :] = row[:, :C]
-        norm_out[0, pl.ds(l, 1), :] = pltpu.roll(row, C, 1)[:, :C]
+        return norms_done(l, jnp.sum(take_stat(rnd, 1), axis=0))
+
+    def norms_done(l, row):
+        norm_out[1, l : l + 1, :] = row[:, :C]
+        norm_out[0, l : l + 1, :] = pltpu.roll(row, C, 1)[:, :C]
         return to_cols(row * total_m)
 
     def grad_z(l, dy, dx):
         n = POS // COLS
         return wide(par[10 + l], n) * (gy_ref[...] - wide(dy, n) - xhat[l] * wide(dx, n))
 
-    def back(t, carry):
-        l = LAYERS - 1 - t
-        sums_start(l, LAYERS + t)
-
-        @pl.when(t > 0)
-        def _():
-            grad_start(l + 1)
-
-        @pl.when(t > 1)
-        def _():
-            grad_back(l + 2)
-
-        sums_cross(LAYERS + t)
-
-        @pl.when(t > 0)
-        def _():
-            grad_cross(l + 1)
-
-        store_taps(grad_z(l, *sums_end(l, LAYERS + t)), g9h, g9l, -1)
+    def input_grad(l, gz):
+        store_taps(gz, g9h, g9l, -1)
         first = mm(wb[l], g9h[...])
-        u_ref[...] = first[:C] + first[C:] + mm(wb[l, :C, :], g9l[...])
-        return carry
-
-    lax.fori_loop(0, LAYERS - 1, back, 0)
-    rnd = 2 * LAYERS - 1
+        return first[:C] + first[C:] + mm(wb[l, :C, :], g9l[...])
+
+    sums_start(3, LAYERS)
+    pair_back()
+    sums_cross(LAYERS)
+    gz = grad_z(3, *sums_end(3, LAYERS))
+    zh[3], zl[3] = split(gz)
+    gy = input_grad(3, gz) * slope[2]
+    gy_ref[...] = gy
+    row_2 = to_row(fold(gy), fold(gy * xhat[2]))
+    gy = input_grad(2, wide(par[12], POS // COLS) * gy) * slope[1]
+    row_1 = to_row(fold(gy), fold(gy * xhat[1]))
+    payload = jnp.concatenate([row_2, row_1], axis=1)
+    for phase in range(2):
+        q_src[phase] = payload
+        q_buf[phase, me[phase]] = payload
+        spread(
+            phase, q_src.at[phase], q_buf.at[phase], q_send.at[phase], q_recv.at[phase], True
+        )
+        (grad_start, grad_cross)[phase](3)
+        settle(phase, q_buf.at[phase], q_recv.at[phase])
+        payload = jnp.sum(q_buf[phase, pl.ds(0, groups[phase])], axis=0)
+    row_2, row_1 = payload[:, :COLS], payload[:, COLS:]
+    dy, dx = norms_done(2, row_2)
+    settle(0, d_full, d_recv.at[2])
+    factors = jnp.concatenate([d_full[i] for i in range(ga)], axis=0)
+    moved = factors * jnp.concatenate([par[12] * dy, par[12] * dx], axis=0)
+    row_1 = row_1 - jnp.sum(moved, axis=0, keepdims=True)
+    gz = grad_z(2, dy, dx)
+    zh[2], zl[2] = split(gz)
+    gy_ref[...] = input_grad(2, gz) * slope[1]
+    gz = grad_z(1, *norms_done(1, row_1))
+    zh[1], zl[1] = split(gz)
+    u_ref[...] = input_grad(1, gz)
+    rnd = LAYERS + 1
     sums_start(0, rnd)
     grad_start(0, *split(gy_ref[...]))
+    grad_start(2)
     grad_start(1)
-    grad_back(2)
+    grad_back(3)
     sums_cross(rnd)
     grad_cross(0)
+    grad_cross(2)
     grad_cross(1)
     settle(1, cx_buf, c_recv.at[1])
     fixed = jnp.sum(cx_buf[...], axis=0)
@@ -624,6 +698,7 @@
         return k_m * (part - fixed[rows:] * dy_m - fixed[:rows] * dx_m)
 
     grad_back(0, finish)
+    grad_back(2)
     grad_back(1)
     gz = grad_z(0, dy, dx)
     for b in range(3):
@@ -643,8 +718,12 @@
 
     for phase in range(2):
         settle(phase, p_buf.at[phase], p_send.at[phase])
-        for r in range(2 * LAYERS):
+        settle(phase, q_buf.at[phase], q_send.at[phase])
+        for r in range(LAYERS + 2):
             settle(phase, s_buf.at[r, phase], s_send.at[r, phase])
+    settle(0, d_buf, d_send.at[0])
+    settle(1, dx_buf, d_send.at[1])
+    settle(0, d_full, d_send.at[2])
     settle(0, c_buf, c_send.at[0])
     settle(1, cx_buf, c_send.at[1])
     for l in range(LAYERS):
@@ -726,8 +805,8 @@
                 pltpu.VMEM((C, POS), F32),
                 pltpu.VMEM((2, 1, 2 * COLS), F32),
                 pltpu.VMEM((2, gmax, 1, 2 * COLS), F32),
-                pltpu.VMEM((2 * LAYERS, 2, 1, COLS), F32),
-                pltpu.VMEM((2 * LAYERS, 2, gmax, 1, COLS), F32),
+                pltpu.VMEM((LAYERS + 2, 2, 1, COLS), F32),
+                pltpu.VMEM((LAYERS + 2, 2, gmax, 1, COLS), F32),
                 pltpu.VMEM((LAYERS, ga, rows, LANES), F32),
                 pltpu.VMEM((LAYERS, ga, rows, LANES), F32),
                 pltpu.VMEM((LAYERS, rows, LANES), F32),
@@ -739,12 +818,26 @@
                 pltpu.VMEM((2 * rows, LANES), F32),
                 pltpu.VMEM((gb, 2 * rows, LANES), F32),
                 pltpu.VMEM((3, ga // CORES, rows, COLS), F32),
+                pltpu.VMEM((LAYERS, C, POS), BF16),
+                pltpu.VMEM((LAYERS, C, POS), BF16),
+                pltpu.VMEM((ga, 2 * C // ga, COLS), F32),
+                pltpu.VMEM((ga, 2 * C // ga, COLS), F32),
+                pltpu.VMEM((2 * C // ga, COLS), F32),
+                pltpu.VMEM((gb, 2 * C // ga, COLS), F32),
+                pltpu.VMEM((2 * C // ga, COLS), F32),
+                pltpu.VMEM((ga, 2 * C // ga, COLS), F32),
+                pltpu.VMEM((2, 1, 2 * COLS), F32),
+                pltpu.VMEM((2, gmax, 1, 2 * COLS), F32),
+                dma((2,)),
+                dma((2,)),
+                dma((3,)),
+                dma((3,)),
                 dma((2,)),
                 dma((2,)),
                 dma((2,)),
                 dma((2,)),
-                dma((2 * LAYERS, 2)),
-                dma((2 * LAYERS, 2)),
+                dma((LAYERS + 2, 2)),
+                dma((LAYERS + 2, 2)),
                 dma((LAYERS, 3)),
                 dma((LAYERS, 3)),
             ],

time: 121 us -> 116 us (0.959)
  Pallas kernels: 120 us -> 115 us
    pallas_call x1, Pallas kernels: 118 us -> 113 us  [per_device(): pl.pallas_call(functools.partial(step_kernel, (nx, ny, nz)), out_shape=(j...]
where the time goes in v3:
time: 116 us
  Pallas kernels  115 us (99%)
    pallas_call x1, Pallas kernels, per_device(): pl.pallas_call(functools.partial(step_kernel, (nx, ny, nz)), out_shape=(j...  113 us

profile of v3, /device:TPU:1, one launch (start us, length us, event | category | flops | bytes accessed | tf_op | source)
XLA Modules:
  0.0 115.9 jit_solution(10749747181535892430)
XLA Ops:
  0.6 113.0 %shard_map.129 = (f32[2,64,4,128]{3,2,1,0:T(4,128)}, f32[9,4,4096]{2,1,0:T(4,128)}, f32[2,4,64]{2,1,0:T(4,128)}, f32[2,64,256]{2,1,0:T(8,128)}) custom-call(f32[2,4,32,256]{3,2,1,0:T(8,128)} %points.1, s32[2,256]{1,0:T(2,128)} %counts.1, s32[2,256]{1,0:T(2,128)} %cells.1, f32[9,64]{1,0:T(8,128)} %pfn_w.1, f32[1,64]{1,0:T(1,128)} %bitcast.5, ...), custom_call_target="tpu_custom_call" | custom-call | tf_op jit(solution)/shard_map/pallas_call | solution.py:776
  113.6 2.1 %shard_map.130 = (f32[2,64,4,128]{3,2,1,0:T(4,128)}, f32[9,4,4096]{2,1,0:T(4,128)}, f32[2,4,64]{2,1,0:T(4,128)}, f32[2,64,256]{2,1,0:T(8,128)}) custom-call(f32[2,64,4,128]{3,2,1,0:T(4,128)} %get-tuple-element.12.refs_0_, f32[9,4,4096]{2,1,0:T(4,128)} %get-tuple-element.13.refs_1_, f32[2,4,64]{2,1,0:T(4,128)} %get-tuple-element.14.refs_2_, ...), custom_call_target="tpu_custom_call" | custom-call | tf_op jit(solution)/shard_map/pallas_call | solution.py:755
